TPU v7x, 32 devices: a whole 2x2x4 slice. The times are simulated.
32 devices in a mesh: group: 4 (over y, x), dp: 8 (over z, core).
Axes of the slice: x: 2, y: 2, z: 4, core: 2. Of those that a mesh axis runs over, the one named last changes fastest.
Arguments:
- observations: bfloat16 [64, 64, 4096], P('dp', None, 'group'), may hold values from -6 to 6
- next_observations: bfloat16 [1024, 4096], P('dp', 'group'), may hold values from -6 to 6
- trunk_weights: bfloat16 [2, 4096, 4096], P(None, 'dp', 'group'), may hold values from -0.125 to 0.125
- head_weights: bfloat16 [4096, 19], P('group'), may hold values from -0.25 to 0.25
- acting_policy_logits: float32 [64, 63, 18], P('dp'), may hold values from -16 to 330, as said below
- actions: int32 [64, 63], P('dp'), may hold values from 0 to 17
- rewards: float32 [64, 63], P('dp'), may hold values from -6 to 6
- episode_finished: int32 [64, 63], P('dp'), may hold values 0 or 1
Outputs:
- trunk_grads: float32 [2, 4096, 4096], P(None, 'dp', 'group')
- head_grads: float32 [4096, 19], P(('group', 'dp'))
- actor_logits: float32 [1024, 18], P('dp')
Inputs may be any that keep to these rules, and one draw needn't show every extreme that they name: `acting_policy_logits`: Real-valued scores, one row for each step and trajectory.
All inputs are finite; a program needn't handle non-finite values. No bound on the sum of `episode_finished` on one device may be relied on, other than what follows from the above.
Results may differ from a plain program's by a relative error of at most 0.012.
Values may be sent and summed in bfloat16 or wider, within the bound.
A program may use at most 128 MiB of HBM per device.

v0:
```python
import jax
import jax.numpy as jnp
from jax import lax
from jax.sharding import PartitionSpec as P

discount_rate = 0.99
value_weight = 0.5
entropy_weight = 0.1
loss_divisor = 16.0


def contract_rows(left, right):
    return lax.dot_general(
        left, right, (((0,), (0,)), ((), ())), preferred_element_type=jnp.float32
    )


def contract_cols(left, right):
    return lax.dot_general(
        left, right, (((1,), (1,)), ((), ())), preferred_element_type=jnp.float32
    )


def silu_slope(pre_value):
    sigma = jax.nn.sigmoid(pre_value)
    return sigma * (1.0 + pre_value * (1.0 - sigma))


def importance_trace_gradients(
    learner_output, acting_policy_logits, actions, rewards, episode_finished
):
    number_of_actions = acting_policy_logits.shape[-1]
    logits = learner_output[:, :, :number_of_actions]
    values = learner_output[:, :, number_of_actions]
    log_policy = jax.nn.log_softmax(logits[:, :-1], axis=-1)
    log_behave = jax.nn.log_softmax(acting_policy_logits, axis=-1)
    chosen = (
        actions[:, :, None] == jnp.arange(number_of_actions, dtype=jnp.int32)[None, None, :]
    ).astype(jnp.float32)
    ratio = jnp.exp(jnp.sum((log_policy - log_behave) * chosen, axis=-1))
    clipped = jnp.minimum(ratio, 1.0)
    discount = discount_rate * (1.0 - episode_finished.astype(jnp.float32))
    current = values[:, :-1]
    following = values[:, 1:]
    deltas = clipped * (rewards + discount * following - current)

    def backward_step(carried, step_item):
        delta_now, factor_now = step_item
        carried = delta_now + factor_now * carried
        return (carried, carried)

    start_carry = jnp.zeros((values.shape[0],), jnp.float32)
    _, corrections = lax.scan(
        backward_step, start_carry, (deltas.T, (discount * clipped).T), reverse=True
    )
    targets = current + corrections.T
    next_targets = jnp.concatenate([targets[:, 1:], values[:, -1:]], axis=1)
    advantage = clipped * (rewards + discount * next_targets - current)
    probability = jnp.exp(log_policy)
    entropy = -jnp.sum(probability * log_policy, axis=-1)
    logit_grad = (
        -advantage[..., None] * (chosen - probability)
        + entropy_weight * probability * (log_policy + entropy[..., None])
    ) / loss_divisor
    value_grad = -value_weight * (targets - current) / loss_divisor
    step_grad = jnp.concatenate([logit_grad, value_grad[..., None]], axis=-1)
    last_row = jnp.zeros((values.shape[0], 1, number_of_actions + 1), jnp.float32)
    return jnp.concatenate([step_grad, last_row], axis=1)


def per_device(
    observations,
    next_observations,
    trunk_weights,
    head_weights,
    acting_policy_logits,
    actions,
    rewards,
    episode_finished,
):
    traj_count, step_count, feature_block = observations.shape
    learner_rows = traj_count * step_count
    number_of_actions = acting_policy_logits.shape[-1]
    layer_total = trunk_weights.shape[0]
    own_rows = observations.reshape(learner_rows, feature_block)
    gathered_weights = [
        lax.all_gather(trunk_weights[layer_index], "dp", axis=0, tiled=True)
        for layer_index in range(layer_total)
    ]
    joined = jnp.concatenate([own_rows, next_observations], axis=0)
    inputs_full = []
    products_block = []
    current = joined
    for forward_layer_index in range(layer_total):
        forward_whole = lax.all_gather(current, "group", axis=1, tiled=True)
        inputs_full.append(forward_whole)
        product = jnp.dot(
            forward_whole, gathered_weights[forward_layer_index], preferred_element_type=jnp.float32
        )
        products_block.append(product)
        current = jax.nn.silu(product).astype(jnp.bfloat16)
    partial_head = jnp.dot(current, head_weights, preferred_element_type=jnp.float32)
    totals = lax.psum(partial_head, "group")
    inputs_full, products_block, last_block, totals = (inputs_full, products_block, current, totals)
    inputs_full = [whole[:learner_rows] for whole in inputs_full]
    products_block = [block[:learner_rows] for block in products_block]
    last_block = last_block[:learner_rows]
    head_out = totals[:learner_rows]
    actor_logits = totals[learner_rows:, :number_of_actions]
    learner_output = head_out.reshape(traj_count, step_count, number_of_actions + 1)
    output_gradient = importance_trace_gradients(
        learner_output, acting_policy_logits, actions, rewards, episode_finished
    )
    output_gradient = output_gradient.reshape(learner_rows, number_of_actions + 1).astype(
        jnp.bfloat16
    )
    head_partial = contract_rows(last_block, output_gradient)
    head_grads = lax.psum_scatter(head_partial, "dp", scatter_dimension=0, tiled=True)
    input_grad = contract_cols(output_gradient, head_weights)
    grad_list = [None] * layer_total
    for layer_index in range(layer_total - 1, -1, -1):
        pre_grad = (input_grad * silu_slope(products_block[layer_index])).astype(jnp.bfloat16)
        all_inputs = lax.all_to_all(
            inputs_full[layer_index], "dp", split_axis=1, concat_axis=0, tiled=True
        )
        all_upstream = lax.all_gather(pre_grad, "dp", axis=0, tiled=True)
        grad_list[layer_index] = contract_rows(all_inputs, all_upstream)
        if layer_index > 0:
            full_grad = contract_cols(pre_grad, gathered_weights[layer_index])
            input_grad = lax.psum_scatter(full_grad, "group", scatter_dimension=1, tiled=True)
    return (jnp.stack(grad_list), head_grads, actor_logits)


def solution(mesh):
    in_specs = (
        P("dp", None, "group"),
        P("dp", "group"),
        P(None, "dp", "group"),
        P("group", None),
        P("dp", None, None),
        P("dp", None),
        P("dp", None),
        P("dp", None),
    )
    out_specs = (P(None, "dp", "group"), P(("group", "dp"), None), P("dp", None))
    return jax.shard_map(
        per_device, mesh=mesh, in_specs=in_specs, out_specs=out_specs, check_vma=False
    )
```

profile of v0, /device:TPU:0, one launch (start us, length us, event | category | flops | bytes accessed | tf_op | source)
XLA Modules:
  0.0 727.3 jit_solution(5411754395285372085)
XLA Ops:
  7.2 2.6 pad_maximum_fusion.1
  9.9 0.0 all-gather.17.cloned.1.call-start
  9.9 1.5 fusion.27
  11.5 0.0 all-gather.19.cloned.1.call-start
  11.5 0.7 all-gather.19.cloned.1.call-update
  12.3 62.2 %all-gather.9.cloned.1.call-done = bf16[640,4096]{1,0:T(8,128)(2,1)} async-done(((bf16[640,1024]{1,0:T(8,128)(2,1)}), bf16[640,4096]{1,0:T(8,128)(2,1)}) %all-gather.9.cloned.1.call-update) | async-done | bytes 5242896 | tf_op jit(solution)/shard_map/all_gather | solution.py:95
  74.5 83.7 %all-gather.17.cloned.1.call-done = bf16[1,4096,1024]{2,1,0:T(8,128)(2,1)} async-done(((bf16[1,512,1024]{2,1,0:T(8,128)(2,1)}), bf16[1,4096,1024]{2,1,0:T(8,128)(2,1)}) %all-gather.17.cloned.1.call-update) | async-done | bytes 8388624 | tf_op jit(solution)/shard_map/all_gather | solution.py:87
  158.1 10.7 %multiply_convert_fusion.1 = (bf16[640,1024]{1,0:T(8,128)(2,1)}, f32[640,1024]{1,0:T(8,128)S(1)}) fusion(bf16[640,4096]{1,0:T(8,128)(2,1)} %all-gather.9.cloned.1.call-done, bf16[1,4096,1024]{2,1,0:T(8,128)(2,1)} %all-gather.17.cloned.1.call-done), kind=kOutput, calls=%fused_computation.12 | convolution fusion | flops 5371985920 | bytes 17563648 | tf_op jit(solution)/shard_map/dot_general | solution.py:97
  168.9 0.0 reduce-scatter.3.cloned.1.call-start
  169.1 71.2 %all-gather.19.cloned.1.call-done = bf16[1,4096,1024]{2,1,0:T(8,128)(2,1)} async-done(((bf16[1,512,1024]{2,1,0:T(8,128)(2,1)}), bf16[1,4096,1024]{2,1,0:T(8,128)(2,1)}) %all-gather.19.cloned.1.call-update) | async-done | bytes 8388624 | tf_op jit(solution)/shard_map/all_gather | solution.py:87
  240.3 62.1 %all-gather.11.cloned.1.call-done = bf16[640,4096]{1,0:T(8,128)(2,1)} async-done(((bf16[640,1024]{1,0:T(8,128)(2,1)}), bf16[640,4096]{1,0:T(8,128)(2,1)}) %all-gather.11.cloned.1.call-update) | async-done | bytes 5242896 | tf_op jit(solution)/shard_map/all_gather | solution.py:95
  302.4 10.9 %multiply_convert_fusion = (bf16[640,1024]{1,0:T(8,128)(2,1)S(1)}, f32[640,1024]{1,0:T(8,128)}) fusion(bf16[640,4096]{1,0:T(8,128)(2,1)} %all-gather.11.cloned.1.call-done, bf16[1,4096,1024]{2,1,0:T(8,128)(2,1)} %all-gather.19.cloned.1.call-done), kind=kOutput, calls=%fused_computation.11 | convolution fusion | flops 5371985920 | bytes 17563648 | tf_op jit(solution)/shard_map/dot_general | solution.py:97
  313.3 1.1 copy-done.3
  314.3 0.4 fusion.28
  314.8 16.2 %psum.7 = f32[640,19]{0,1:T(8,128)S(1)} all-reduce(f32[640,19]{0,1:T(8,128)S(1)} %fusion.28), channel_id=1, replica_groups=mesh['group'=4,'dp'=8] {'group'}, use_global_device_ids=true, to_apply=%region_0.1 | all-reduce | flops 12160 | bytes 97280 | tf_op jit(solution)/shard_map/psum | solution.py:103
  331.0 0.1 reshape.32
  331.2 0.1 slice.56
  331.3 0.1 multiply_bitcast_fusion
  331.3 0.1 copy.50
  331.4 0.1 copy.49
  331.5 4.7 while.17
  336.3 0.1 copy.51
  336.4 0.1 slice.55
  336.4 0.1 fusion.25
  336.6 0.1 convert_element_type.26
  336.7 3.4 multiply_convert_fusion.3
  340.1 11.5 %fusion.2 = f32[512,4096]{1,0:T(8,128)} fusion(bf16[512,1024]{1,0:T(8,128)(2,1)} %multiply_convert_fusion.3, bf16[1,4096,1024]{2,1,0:T(8,128)(2,1)} %all-gather.19.cloned.1.call-done), kind=kOutput, calls=%fused_computation.3 | convolution fusion | flops 4294967296 | bytes 17825792 | tf_op jit(solution)/shard_map/dot_general | solution.py:19
  351.7 0.5 all-gather.15.cloned.1.call-update
  352.3 4.7 slice.62
  357.0 6.6 copy.47
  363.6 4.6 all-to-all-start
  368.2 0.2 all-gather.13.cloned.1.call-start
  368.4 69.6 %reduce-scatter.3.cloned.1.call-done = f32[512,1024]{1,0:T(8,128)} async-done(((f32[512,4096]{1,0:T(8,128)}), f32[512,1024]{1,0:T(8,128)}) %reduce-scatter.3.cloned.1.call-update) | async-done | bytes 2097168 | tf_op jit(solution)/shard_map/reduce_scatter | solution.py:130
  438.0 3.3 multiply_convert_fusion.2
  441.3 2.2 slice-done
  443.5 2.4 copy.55
  445.9 50.0 %all-to-all-done = bf16[512,8,512]{0,2,1:T(8,128)(2,1)} async-done(((bf16[512,8,512]{0,2,1:T(8,128)(2,1)}), bf16[512,8,512]{0,2,1:T(8,128)(2,1)}, u32[]{:S(2)}, u32[]{:S(2)}) %all-to-all-start) | async-done | bytes 4194336 | tf_op jit(solution)/shard_map/all_to_all | solution.py:123
  495.9 4.6 all-to-all-start.1
  500.5 0.0 reduce-scatter.5.cloned.1.call-start
  500.5 6.6 copy.48
  507.2 0.6 slice.70
  507.8 0.9 fusion.8
  508.7 146.3 %all-to-all-done.1 = bf16[512,8,512]{2,0,1:T(8,128)(2,1)} async-done(((bf16[512,8,512]{2,0,1:T(8,128)(2,1)}), bf16[512,8,512]{2,0,1:T(8,128)(2,1)}, u32[]{:S(2)}, u32[]{:S(2)}) %all-to-all-start.1) | async-done | bytes 4194336 | tf_op jit(solution)/shard_map/all_to_all | solution.py:123
  655.0 8.3 %convolution_bitcast_fusion = f32[1,512,1024]{2,1,0:T(8,128)S(1)} fusion(bf16[4096,512]{1,0:T(8,128)(2,1)} %bitcast.13, bf16[4096,1024]{1,0:T(8,128)(2,1)} %all-gather.15.cloned.1.call-done), kind=kOutput, calls=%fused_computation.15 | convolution fusion | flops 4294967296 | bytes 14680064 | tf_op jit(solution)/shard_map/dot_general | solution.py:13
  663.3 26.0 %all-gather.13.cloned.1.call-done = bf16[4096,1024]{1,0:T(8,128)(2,1)} async-done(((bf16[512,1024]{1,0:T(8,128)(2,1)}), bf16[4096,1024]{1,0:T(8,128)(2,1)}) %all-gather.13.cloned.1.call-update) | async-done | bytes 8388624 | tf_op jit(solution)/shard_map/all_gather | solution.py:126
  689.3 8.2 %convolution_bitcast_fusion.1 = f32[1,512,1024]{2,1,0:T(8,128)S(1)} fusion(bf16[4096,512]{1,0:T(8,128)(2,1)} %bitcast.68, bf16[4096,1024]{1,0:T(8,128)(2,1)} %all-gather.13.cloned.1.call-done), kind=kOutput, calls=%fused_computation.16 | convolution fusion | flops 4294967296 | bytes 14680064 | tf_op jit(solution)/shard_map/dot_general | solution.py:13
  697.5 2.5 pad_maximum_fusion
  700.0 20.5 %reduce-scatter.5.cloned.1.call-done = f32[128,19]{0,1:T(8,128)} async-done(((f32[1024,19]{0,1:T(8,128)}), f32[128,19]{0,1:T(8,128)}) %reduce-scatter.5.cloned.1.call-update) | async-done | bytes 9744 | tf_op jit(solution)/shard_map/reduce_scatter | solution.py:118
  (169 shorter events, 4.2 us)
Async XLA Ops:
  7.2 307.2 %copy-start = (bf16[1024,19]{0,1:T(8,128)(2,1)S(1)}, bf16[1024,19]{0,1:T(8,128)(2,1)}, u32[]{:S(2)}) copy-start(bf16[1024,19]{0,1:T(8,128)(2,1)} %param.14) | copy-start | bytes 116740
  7.2 2.7 copy-start.2
  7.2 67.3 %all-gather.9.cloned.1.call-start = ((), (), s32[]{:S(2)}) async-start(), calls=%async_computation.4 | async-start | bytes 6553600 | tf_op jit(solution)/shard_map/all_gather | solution.py:95
  9.9 148.3 %all-gather.17.cloned.1.call-start = ((), (), s32[]{:S(2)}) async-start(), calls=%async_computation.10 | async-start | bytes 9437184 | tf_op jit(solution)/shard_map/all_gather | solution.py:87
  11.5 228.8 %all-gather.19.cloned.1.call-start = ((), (), s32[]{:S(2)}) async-start(), calls=%async_computation.11 | async-start | bytes 9437184 | tf_op jit(solution)/shard_map/all_gather | solution.py:87
  12.2 156.8 %copy-start.5 = (f32[8,63,18]{1,0,2:T(8,128)S(1)}, f32[8,63,18]{1,0,2:T(8,128)}, u32[]{:S(2)}) copy-start(f32[8,63,18]{1,0,2:T(8,128)} %param.15) | copy-start | bytes 108868
  12.2 290.2 %all-gather.11.cloned.1.call-start = ((), (), s32[]{:S(2)}) async-start(), calls=%async_computation.5 | async-start | bytes 6553600 | tf_op jit(solution)/shard_map/all_gather | solution.py:95
  168.9 269.1 %reduce-scatter.3.cloned.1.call-start = ((), (), s32[]{:S(2)}) async-start(), calls=%async_computation.6 | async-start | bytes 10485760 | tf_op jit(solution)/shard_map/reduce_scatter | solution.py:130
  169.0 162.1 %copy-start.8 = (s32[8,63]{1,0:T(8,128)S(1)}, s32[8,63]{1,0:T(8,128)}, u32[]{:S(2)}) copy-start(s32[8,63]{1,0:T(8,128)} %param.16) | copy-start | bytes 6052
  169.0 162.2 %copy-start.6 = (s32[8,63]{1,0:T(8,128)S(1)}, s32[8,63]{1,0:T(8,128)}, u32[]{:S(2)}) copy-start(s32[8,63]{1,0:T(8,128)} %param.18) | copy-start | bytes 6052
  169.0 162.2 %copy-start.7 = (f32[8,63]{1,0:T(8,128)S(1)}, f32[8,63]{1,0:T(8,128)}, u32[]{:S(2)}) copy-start(f32[8,63]{1,0:T(8,128)} %param.17) | copy-start | bytes 6052
  313.3 1.1 copy-start.3
  351.7 303.3 %all-gather.15.cloned.1.call-start = ((), (), s32[]{:S(2)}) async-start(), calls=%async_computation.8 | async-start | bytes 9437184 | tf_op jit(solution)/shard_map/all_gather | solution.py:126
  363.6 132.3 %all-to-all-start = ((bf16[512,8,512]{0,2,1:T(8,128)(2,1)}), bf16[512,8,512]{0,2,1:T(8,128)(2,1)}, u32[]{:S(2)}, u32[]{:S(2)}) async-start(bf16[512,8,512]{0,2,1:T(8,128)(2,1)} %bitcast.65), calls=%async_computation | async-start | bytes 8388608 | tf_op jit(solution)/shard_map/all_to_all | solution.py:123
  368.2 321.1 %all-gather.13.cloned.1.call-start = ((), (), s32[]{:S(2)}) async-start(), calls=%async_computation.7 | async-start | bytes 9437184 | tf_op jit(solution)/shard_map/all_gather | solution.py:126
  441.3 2.2 slice-start
  495.9 159.1 %all-to-all-start.1 = ((bf16[512,8,512]{2,0,1:T(8,128)(2,1)}), bf16[512,8,512]{2,0,1:T(8,128)(2,1)}, u32[]{:S(2)}, u32[]{:S(2)}) async-start(bf16[512,8,512]{2,0,1:T(8,128)(2,1)} %bitcast.66), calls=%async_computation.2 | async-start | bytes 8388608 | tf_op jit(solution)/shard_map/all_to_all | solution.py:123
  500.5 220.0 %reduce-scatter.5.cloned.1.call-start = ((), (), s32[]{:S(2)}) async-start(), calls=%async_computation.9 | async-start | bytes 110592 | tf_op jit(solution)/shard_map/reduce_scatter | solution.py:118
  500.5 7.3 copy-start.4
  689.3 31.2 %copy-start.1 = (bf16[1024,19]{0,1:T(8,128)(2,1)S(1)}, bf16[1024,19]{0,1:T(8,128)(2,1)}, u32[]{:S(2)}) copy-start(bf16[1024,19]{0,1:T(8,128)(2,1)} %param.14) | copy-start | bytes 116740
Sparse Core Ops, SparseCore 0:
  10.4 64.0 all-gather.8
  76.1 82.0 all-gather.16
  159.7 80.5 all-gather.18
  242.6 59.7 all-gather.10
  351.8 86.1 reduce-scatter.2
  439.4 153.6 all-gather.14
  594.7 94.5 all-gather.12
  692.1 28.3 reduce-scatter.4
where the time goes:
time: 728 us; the launch traced here: 727 us
  waiting for transfers between devices  593 us (81%)
  matrix products  54.4 us (7%)
  local copies, waits for them, and re-layouts  28.9 us (4%)
  blocking collectives  16.2 us (2%)
  between operations  14.3 us (2%)
  other arithmetic  9.97 us (1%)
  starting transfers between devices  9.68 us (1%)
    all_to_all x2, waiting for transfers between devices, per_device(): lax.all_to_all(inputs_full[layer_index], 'dp', split_axis=1, concat_axis=...  196 us
    all_gather x2, waiting for transfers between devices, per_device(): lax.all_gather(trunk_weights[layer_index], 'dp', axis=0, tiled=True)  155 us
    all_gather x2, waiting for transfers between devices, per_device(): forward_whole = lax.all_gather(current, 'group', axis=1, tiled=True)  124 us
    reduce_scatter x1, waiting for transfers between devices, per_device(): lax.psum_scatter(full_grad, 'group', scatter_dimension=1, tiled=True)  69.6 us
    all_gather x2, waiting for transfers between devices, per_device(): all_upstream = lax.all_gather(pre_grad, 'dp', axis=0, tiled=True)  26 us
    dot_general x2, matrix products, per_device(): jnp.dot(forward_whole, gathered_weights[forward_layer_index], preferred_e...  21.6 us
    reduce_scatter x1, waiting for transfers between devices, per_device(): lax.psum_scatter(head_partial, 'dp', scatter_dimension=0, tiled=True)  20.5 us
    dot_general x3, matrix products, contract_rows(): lax.dot_general(left, right, (((0,), (0,)), ((), ())), preferred_element_...  17.4 us
  transfers between devices with their start and end apart: 10, of which 9 were waited for; matrix products, arithmetic and copies ran while one was open for 8% of the time, Pallas kernels for 0%

commit v1 on v0

--- a/solution.py
+++ b/solution.py
@@ -7,6 +7,13 @@
 value_weight = 0.5
 entropy_weight = 0.1
 loss_divisor = 16.0
+
+
+def exchange_gather(block, axis, dim):
+    size = lax.axis_size(axis)
+    pieces = jnp.stack([block for _ in range(size)])
+    pieces = lax.all_to_all(pieces, axis, split_axis=0, concat_axis=0)
+    return jnp.concatenate(pieces, axis=dim)
 
 
 def contract_rows(left, right):
@@ -84,8 +91,7 @@
     layer_total = trunk_weights.shape[0]
     own_rows = observations.reshape(learner_rows, feature_block)
     gathered_weights = [
-        lax.all_gather(trunk_weights[layer_index], "dp", axis=0, tiled=True)
-        for layer_index in range(layer_total)
+        exchange_gather(trunk_weights[layer_index], "dp", 0) for layer_index in range(layer_total)
     ]
     joined = jnp.concatenate([own_rows, next_observations], axis=0)
     inputs_full = []

time: 728 us -> 823 us (1.13)
  waiting for transfers between devices: 593 us -> 667 us
  starting transfers between devices: 9.68 us -> 20.9 us
  local copies, waits for them, and re-layouts: 28.9 us -> 37.7 us
    all_to_all x0 -> x2, waiting for transfers between devices: none -> 356 us  [exchange_gather(): pieces = lax.all_to_all(pieces, axis, split_axis=0, concat_axis=0)]
    all_gather x2 -> x0, waiting for transfers between devices: 155 us -> none  [per_device(): lax.all_gather(trunk_weights[layer_index], 'dp', axis=0, tiled=True)]
    all_gather x2, waiting for transfers between devices: 124 us -> 0.02 us  [per_device(): forward_whole = lax.all_gather(current, 'group', axis=1, tiled=True)]
    all_to_all x2, waiting for transfers between devices: 196 us -> 209 us  [per_device(): lax.all_to_all(inputs_full[layer_index], 'dp', split_axis=1, concat_axis=...]
    all_to_all x0 -> x2, starting transfers between devices: none -> 11.4 us  [exchange_gather(): pieces = lax.all_to_all(pieces, axis, split_axis=0, concat_axis=0)]
    all_gather x2, waiting for transfers between devices: 26 us -> 15.6 us  [per_device(): all_upstream = lax.all_gather(pre_grad, 'dp', axis=0, tiled=True)]
    another operation x0 -> x2, local copies, waits for them, and re-layouts: none -> 8.63 us  [exchange_gather(): pieces = jnp.stack([block for _ in range(size)])]
  transfers between devices with their start and end apart: 10 -> 10, of which waited for: 9 -> 7; matrix products, arithmetic and copies ran while one was open for 8% -> 7% of each run, Pallas kernels for 0% -> 0%
where the time goes in v1:
time: 823 us; the launch traced here: 822 us
  waiting for transfers between devices  667 us (81%)
  matrix products  54.5 us (7%)
  local copies, waits for them, and re-layouts  37.7 us (5%)
  starting transfers between devices  20.9 us (3%)
  blocking collectives  17.2 us (2%)
  between operations  14.3 us (2%)
  other arithmetic  8.51 us (1%)
    all_to_all x2, waiting for transfers between devices, exchange_gather(): pieces = lax.all_to_all(pieces, axis, split_axis=0, concat_axis=0)  356 us
    all_to_all x2, waiting for transfers between devices, per_device(): lax.all_to_all(inputs_full[layer_index], 'dp', split_axis=1, concat_axis=...  209 us
    reduce_scatter x1, waiting for transfers between devices, per_device(): lax.psum_scatter(full_grad, 'group', scatter_dimension=1, tiled=True)  66.9 us
    dot_general x2, matrix products, per_device(): jnp.dot(forward_whole, gathered_weights[forward_layer_index], preferred_e...  21.7 us
    reduce_scatter x1, waiting for transfers between devices, per_device(): lax.psum_scatter(head_partial, 'dp', scatter_dimension=0, tiled=True)  19.7 us
    dot_general x3, matrix products, contract_rows(): lax.dot_general(left, right, (((0,), (0,)), ((), ())), preferred_element_...  17.5 us
    psum x1, blocking collectives, per_device(): totals = lax.psum(partial_head, 'group')  17.2 us
  transfers between devices with their start and end apart: 10, of which 7 were waited for; matrix products, arithmetic and copies ran while one was open for 7% of the time, Pallas kernels for 0%

profile of v1, /device:TPU:0, one launch (start us, length us, event | category | flops | bytes accessed | tf_op | source)
XLA Modules:
  0.0 821.7 jit_solution(2879486630404839702)
XLA Ops:
  7.2 1.7 slice_bitcast_fusion
  8.9 4.3 stack.15
  13.2 6.5 all-to-all-start.1
  19.8 1.2 pad_maximum_fusion.1
  20.9 182.7 %all-to-all-done.1 = bf16[8,512,1024]{2,1,0:T(8,128)(2,1)} async-done(((bf16[8,512,1024]{2,1,0:T(8,128)(2,1)}), bf16[8,512,1024]{2,1,0:T(8,128)(2,1)}, u32[]{:S(2)}, u32[]{:S(2)}) %all-to-all-start.1) | async-done | bytes 8388640 | tf_op jit(solution)/shard_map/all_to_all | solution.py:15
  203.7 4.3 stack.16
  208.0 5.0 all-to-all-start.2
  213.0 0.0 all-gather.7.cloned.1.call-start
  213.0 10.8 %multiply_convert_fusion.1 = (bf16[640,1024]{1,0:T(8,128)(2,1)}, f32[640,1024]{1,0:T(8,128)S(1)}) fusion(bf16[640,4096]{1,0:T(8,128)(2,1)} %all-gather.5.cloned.1.call-done, bf16[4096,1024]{1,0:T(8,128)(2,1)} %bitcast.5), kind=kOutput, calls=%fused_computation.6 | convolution fusion | flops 5371985920 | bytes 17563648 | tf_op jit(solution)/shard_map/dot_general | solution.py:103
  223.8 0.0 reduce-scatter.3.cloned.1.call-start
  224.0 172.8 %all-to-all-done.2 = bf16[8,512,1024]{2,1,0:T(8,128)(2,1)} async-done(((bf16[8,512,1024]{2,1,0:T(8,128)(2,1)}), bf16[8,512,1024]{2,1,0:T(8,128)(2,1)}, u32[]{:S(2)}, u32[]{:S(2)}) %all-to-all-start.2) | async-done | bytes 8388640 | tf_op jit(solution)/shard_map/all_to_all | solution.py:15
  396.8 10.9 %multiply_convert_fusion = (bf16[640,1024]{1,0:T(8,128)(2,1)S(1)}, f32[640,1024]{1,0:T(8,128)}) fusion(bf16[640,4096]{1,0:T(8,128)(2,1)} %all-gather.7.cloned.1.call-done, bf16[4096,1024]{1,0:T(8,128)(2,1)} %bitcast.7), kind=kOutput, calls=%fused_computation.5 | convolution fusion | flops 5371985920 | bytes 17563648 | tf_op jit(solution)/shard_map/dot_general | solution.py:103
  407.7 1.1 copy-done.2
  408.8 0.4 fusion.21
  409.2 17.2 %psum.7 = f32[640,19]{0,1:T(8,128)S(1)} all-reduce(f32[640,19]{0,1:T(8,128)S(1)} %fusion.21), channel_id=1, replica_groups=mesh['group'=4,'dp'=8] {'group'}, use_global_device_ids=true, to_apply=%region_0.1 | all-reduce | flops 12160 | bytes 97280 | tf_op jit(solution)/shard_map/psum | solution.py:109
  426.5 0.1 reshape.42
  426.6 0.1 slice.62
  426.8 0.1 multiply_bitcast_fusion
  426.8 0.1 copy.49
  426.9 0.1 copy.50
  427.0 4.7 while.17
  431.8 0.1 copy.51
  431.9 0.1 slice.61
  431.9 0.1 fusion.19
  432.1 0.1 convert_element_type.26
  432.2 3.5 multiply_convert_fusion.3
  435.6 11.5 %fusion.22 = f32[512,4096]{1,0:T(8,128)} fusion(bf16[512,1024]{1,0:T(8,128)(2,1)} %multiply_convert_fusion.3, bf16[4096,1024]{1,0:T(8,128)(2,1)} %bitcast.7), kind=kOutput, calls=%fused_computation.52 | convolution fusion | flops 4294967296 | bytes 17825792 | tf_op jit(solution)/shard_map/dot_general | solution.py:26
  447.2 0.0 all-gather.11.cloned.1.call-start
  447.2 0.5 all-gather.11.cloned.1.call-update
  447.7 4.7 slice.68
  452.4 6.6 copy.47
  459.0 4.6 all-to-all-start
  463.7 66.9 %reduce-scatter.3.cloned.1.call-done = f32[512,1024]{1,0:T(8,128)} async-done(((f32[512,4096]{1,0:T(8,128)}), f32[512,1024]{1,0:T(8,128)}) %reduce-scatter.3.cloned.1.call-update) | async-done | bytes 2097168 | tf_op jit(solution)/shard_map/reduce_scatter | solution.py:136
  530.5 3.3 multiply_convert_fusion.2
  533.9 2.2 slice-done
  536.1 2.4 copy.55
  538.5 55.4 %all-to-all-done = bf16[512,8,512]{0,2,1:T(8,128)(2,1)} async-done(((bf16[512,8,512]{0,2,1:T(8,128)(2,1)}), bf16[512,8,512]{0,2,1:T(8,128)(2,1)}, u32[]{:S(2)}, u32[]{:S(2)}) %all-to-all-start) | async-done | bytes 4194336 | tf_op jit(solution)/shard_map/all_to_all | solution.py:129
  593.9 4.6 all-to-all-start.3
  598.5 0.0 reduce-scatter.5.cloned.1.call-start
  598.6 6.7 copy.48
  605.3 0.6 slice.76
  605.9 0.9 fusion.2
  606.8 153.7 %all-to-all-done.3 = bf16[512,8,512]{2,0,1:T(8,128)(2,1)} async-done(((bf16[512,8,512]{2,0,1:T(8,128)(2,1)}), bf16[512,8,512]{2,0,1:T(8,128)(2,1)}, u32[]{:S(2)}, u32[]{:S(2)}) %all-to-all-start.3) | async-done | bytes 4194336 | tf_op jit(solution)/shard_map/all_to_all | solution.py:129
  760.5 8.4 %convolution_bitcast_fusion = f32[1,512,1024]{2,1,0:T(8,128)S(1)} fusion(bf16[4096,512]{1,0:T(8,128)(2,1)} %bitcast.15, bf16[4096,1024]{1,0:T(8,128)(2,1)} %all-gather.11.cloned.1.call-done), kind=kOutput, calls=%fused_computation.9 | convolution fusion | flops 4294967296 | bytes 14680064 | tf_op jit(solution)/shard_map/dot_general | solution.py:20
  768.9 15.6 %all-gather.9.cloned.1.call-done = bf16[4096,1024]{1,0:T(8,128)(2,1)} async-done(((bf16[512,1024]{1,0:T(8,128)(2,1)}), bf16[4096,1024]{1,0:T(8,128)(2,1)}) %all-gather.9.cloned.1.call-update) | async-done | bytes 8388624 | tf_op jit(solution)/shard_map/all_gather | solution.py:132
  784.4 8.2 convolution_bitcast_fusion.1
  792.7 2.5 pad_maximum_fusion
  795.1 19.7 %reduce-scatter.5.cloned.1.call-done = f32[128,19]{0,1:T(8,128)} async-done(((f32[1024,19]{0,1:T(8,128)}), f32[128,19]{0,1:T(8,128)}) %reduce-scatter.5.cloned.1.call-update) | async-done | bytes 9744 | tf_op jit(solution)/shard_map/reduce_scatter | solution.py:124
  (171 shorter events, 4.1 us)
Async XLA Ops:
  7.2 401.6 %copy-start = (bf16[1024,19]{0,1:T(8,128)(2,1)S(1)}, bf16[1024,19]{0,1:T(8,128)(2,1)}, u32[]{:S(2)}) copy-start(bf16[1024,19]{0,1:T(8,128)(2,1)} %param.14) | copy-start | bytes 116740
  13.2 6.5 copy-start.4
  13.2 6.5 copy-start.6
  13.2 190.4 %all-to-all-start.1 = ((bf16[8,512,1024]{2,1,0:T(8,128)(2,1)}), bf16[8,512,1024]{2,1,0:T(8,128)(2,1)}, u32[]{:S(2)}, u32[]{:S(2)}) async-start(bf16[8,512,1024]{2,1,0:T(8,128)(2,1)} %stack.15), calls=%async_computation.1 | async-start | bytes 16777216 | tf_op jit(solution)/shard_map/all_to_all | solution.py:15
  19.7 193.3 %all-gather.5.cloned.1.call-start = ((), (), s32[]{:S(2)}) async-start(), calls=%async_computation.6 | async-start | bytes 6553600 | tf_op jit(solution)/shard_map/all_gather | solution.py:101
  208.0 188.8 %all-to-all-start.2 = ((bf16[8,512,1024]{2,1,0:T(8,128)(2,1)}), bf16[8,512,1024]{2,1,0:T(8,128)(2,1)}, u32[]{:S(2)}, u32[]{:S(2)}) async-start(bf16[8,512,1024]{2,1,0:T(8,128)(2,1)} %stack.16), calls=%async_computation.2 | async-start | bytes 16777216 | tf_op jit(solution)/shard_map/all_to_all | solution.py:15
  213.0 183.9 %all-gather.7.cloned.1.call-start = ((), (), s32[]{:S(2)}) async-start(), calls=%async_computation.7 | async-start | bytes 6553600 | tf_op jit(solution)/shard_map/all_gather | solution.py:101
  213.0 10.9 %copy-start.5 = (f32[8,63,18]{1,0,2:T(8,128)S(1)}, f32[8,63,18]{1,0,2:T(8,128)}, u32[]{:S(2)}) copy-start(f32[8,63,18]{1,0,2:T(8,128)} %param.15) | copy-start | bytes 108868
  223.8 306.7 %reduce-scatter.3.cloned.1.call-start = ((), (), s32[]{:S(2)}) async-start(), calls=%async_computation.8 | async-start | bytes 10485760 | tf_op jit(solution)/shard_map/reduce_scatter | solution.py:136
  396.8 29.9 %copy-start.9 = (s32[8,63]{1,0:T(8,128)S(1)}, s32[8,63]{1,0:T(8,128)}, u32[]{:S(2)}) copy-start(s32[8,63]{1,0:T(8,128)} %param.16) | copy-start | bytes 6052
  396.8 29.9 %copy-start.7 = (s32[8,63]{1,0:T(8,128)S(1)}, s32[8,63]{1,0:T(8,128)}, u32[]{:S(2)}) copy-start(s32[8,63]{1,0:T(8,128)} %param.18) | copy-start | bytes 6052
  396.8 29.9 %copy-start.8 = (f32[8,63]{1,0:T(8,128)S(1)}, f32[8,63]{1,0:T(8,128)}, u32[]{:S(2)}) copy-start(f32[8,63]{1,0:T(8,128)} %param.17) | copy-start | bytes 6052
  407.7 1.1 copy-start.2
  447.2 313.3 %all-gather.11.cloned.1.call-start = ((), (), s32[]{:S(2)}) async-start(), calls=%async_computation.10 | async-start | bytes 9437184 | tf_op jit(solution)/shard_map/all_gather | solution.py:132
  459.0 134.9 %all-to-all-start = ((bf16[512,8,512]{0,2,1:T(8,128)(2,1)}), bf16[512,8,512]{0,2,1:T(8,128)(2,1)}, u32[]{:S(2)}, u32[]{:S(2)}) async-start(bf16[512,8,512]{0,2,1:T(8,128)(2,1)} %bitcast.62), calls=%async_computation | async-start | bytes 8388608 | tf_op jit(solution)/shard_map/all_to_all | solution.py:129
  463.6 320.8 %all-gather.9.cloned.1.call-start = ((), (), s32[]{:S(2)}) async-start(), calls=%async_computation.9 | async-start | bytes 9437184 | tf_op jit(solution)/shard_map/all_gather | solution.py:132
  533.9 2.2 slice-start
  593.9 166.6 %all-to-all-start.3 = ((bf16[512,8,512]{2,0,1:T(8,128)(2,1)}), bf16[512,8,512]{2,0,1:T(8,128)(2,1)}, u32[]{:S(2)}, u32[]{:S(2)}) async-start(bf16[512,8,512]{2,0,1:T(8,128)(2,1)} %bitcast.63), calls=%async_computation.4 | async-start | bytes 8388608 | tf_op jit(solution)/shard_map/all_to_all | solution.py:129
  598.5 216.3 %reduce-scatter.5.cloned.1.call-start = ((), (), s32[]{:S(2)}) async-start(), calls=%async_computation.11 | async-start | bytes 110592 | tf_op jit(solution)/shard_map/reduce_scatter | solution.py:124
  598.6 7.3 copy-start.3
  784.4 30.4 %copy-start.1 = (bf16[1024,19]{0,1:T(8,128)(2,1)S(1)}, bf16[1024,19]{0,1:T(8,128)(2,1)}, u32[]{:S(2)}) copy-start(bf16[1024,19]{0,1:T(8,128)(2,1)} %param.14) | copy-start | bytes 116740
Sparse Core Ops, SparseCore 0:
  22.9 62.7 all-gather.4
  224.0 62.6 all-gather.6
  447.3 83.1 reduce-scatter.2
  532.0 156.2 all-gather.10
  689.7 94.6 all-gather.8
  787.1 27.6 reduce-scatter.4
